TPU v7x, 32 devices: a whole 2x2x4 slice. The times are simulated.
32 devices in a mesh: dom: 8 (over z, x), sub: 4 (over y, core).
Axes of the slice: x: 2, y: 2, z: 4, core: 2. Of those that a mesh axis runs over, the one named last changes fastest.
Arguments:
- load_vector: float32 [64, 128], P(('dom', 'sub')), may hold values from -38 to 38
- recycled: float32 [40, 64, 128], P(None, ('dom', 'sub')), may hold values from -6 to 6
- images: float32 [40, 64, 128], P(None, ('dom', 'sub')), may hold values from -6 to 6
- matrix_tiles: float32 [64, 8, 128, 128], P(('dom', 'sub')), may hold values from -7 to 7
- tile_columns: int32 [64, 8], P(('dom', 'sub')), may hold values from 0 to 5, as said below
- ghost_list: int32 [32, 4], P(('dom', 'sub')), may hold values from 0 to 23, as said below
- live_counts: int32 [32], P(('dom', 'sub')), may hold values from 1 to 2, as said below
Outputs:
- solution: float32 [64, 128], P(('dom', 'sub'))
- residual: float32 [64, 128], P(('dom', 'sub'))
Inputs may be any that keep to these rules, and one draw needn't show every extreme that they name: `live_counts`: each device's live block rows are its first slots; some device has all 2 live. `tile_columns`: tile 0 of a block row names the row's own slot. Other entries below 2 name a live slot of the same device; entries from 2 on name a ghost slot of that device. `ghost_list`: each entry names a live slot q of a device with sub index s and dom index differing from the owner's by o - 1 (o of 0, 1, 2), coded as o * (size of sub) * 2 + s * 2 + q; it never points outside the dom axis and never to the owner itself.
All inputs are finite; a program needn't handle non-finite values.
Results may differ from a plain program's by a relative error of at most 0.0003.
Values sent between devices are 32-bit elements; how exact they have to be, the bound alone decides.
No kernel may reach another device: no remote copies, remote signals or barrier semaphores. Data moves between devices by JAX's collectives and lax.ppermute only.
A program may use at most 64 MiB of HBM per device.

v0:
```python
import jax
import jax.numpy as jnp
from jax import lax
from jax.sharding import PartitionSpec as P

STEPS = 3


def padded(value, sides, width):
    for axis, dim in sides:
        count, length = (lax.axis_size(axis), value.shape[dim])
        up = [(i, (i + 1) % count) for i in range(count - 1)]
        down = [(j, i) for i, j in up]
        last = lax.slice_in_dim(value, length - width, length, axis=dim)
        first = lax.slice_in_dim(value, 0, width, axis=dim)
        before = lax.ppermute(last, axis, up)
        after = lax.ppermute(first, axis, down)
        value = jnp.concatenate([before, value, after], axis=dim)
    return value


def triangle_solve(factor, values, transpose):
    column = values if values.ndim == 2 else values[:, None]
    solved = lax.linalg.triangular_solve(
        factor, column, left_side=True, lower=True, transpose_a=transpose
    )
    return solved if values.ndim == 2 else solved[:, 0]


def multiply(vector, matrix_tiles, tile_columns, ghost_codes):
    slot_count = vector.shape[0]
    group_size = lax.axis_size("sub") * slot_count
    gathered = lax.all_gather(vector, "sub", axis=0, tiled=True)
    nearby = padded(gathered, (("dom", 0),), group_size)
    ghosts = jnp.take(nearby, ghost_codes, axis=0)
    extended = jnp.concatenate([vector, ghosts], axis=0)
    picked = jnp.take(extended, tile_columns, axis=0)
    return jnp.einsum("stij,stj->si", matrix_tiles, picked, precision=lax.Precision.HIGHEST)


def local(load_vector, recycled, images, matrix_tiles, tile_columns, ghost_list, live_counts):
    highest = lax.Precision.HIGHEST
    slot_count, tile_width = load_vector.shape
    recycled_count = recycled.shape[0]
    live_mask = (jnp.arange(slot_count) < live_counts[0]).astype(jnp.float32)[:, None]
    ghost_codes = ghost_list[0]
    source = (load_vector * live_mask).reshape(-1)
    recycled_flat = (recycled * live_mask[None]).reshape(recycled_count, -1)
    images_flat = (images * live_mask[None]).reshape(recycled_count, -1)
    gram_matrix, projection, source_norm = lax.psum(
        (
            jnp.dot(images_flat, images_flat.T, precision=highest),
            jnp.dot(images_flat, source, precision=highest),
            jnp.sum(source * source),
        ),
        ("dom", "sub"),
    )
    cholesky_low = jnp.linalg.cholesky(gram_matrix)
    reduced = triangle_solve(cholesky_low, projection, False)
    initial_norm = jnp.sqrt(source_norm - jnp.sum(reduced * reduced))
    images_hat = triangle_solve(cholesky_low, images_flat, False)
    recycled_hat = triangle_solve(cholesky_low, recycled_flat, False)
    start_point = jnp.dot(reduced, recycled_hat, precision=highest)
    start_residual = source - jnp.dot(reduced, images_hat, precision=highest)
    basis = [start_residual / initial_norm]
    hessenberg = jnp.zeros((STEPS + 1, STEPS), jnp.float32)
    coupling = jnp.zeros((recycled_count, STEPS), jnp.float32)
    for column in range(STEPS):
        image_now = multiply(
            basis[column].reshape(slot_count, tile_width), matrix_tiles, tile_columns, ghost_codes
        )
        image_now = (image_now * live_mask).reshape(-1)
        stacked = jnp.stack(basis)
        local_images = jnp.dot(images_hat, image_now, precision=highest)
        summed_images, against_basis, image_norm = lax.psum(
            (
                local_images,
                jnp.dot(stacked, image_now, precision=highest),
                jnp.sum(image_now * image_now),
            ),
            ("dom", "sub"),
        )
        correction = jnp.dot(summed_images, images_hat, precision=highest)
        next_norm = jnp.sqrt(
            image_norm
            - jnp.sum(summed_images * summed_images)
            - jnp.sum(against_basis * against_basis)
        )
        remaining = image_now - correction - jnp.dot(against_basis, stacked, precision=highest)
        basis.append(remaining / next_norm)
        hessenberg = hessenberg.at[: column + 1, column].set(against_basis)
        hessenberg = hessenberg.at[column + 1, column].set(next_norm)
        coupling = coupling.at[:, column].set(summed_images)
    normal_matrix = jnp.dot(hessenberg.T, hessenberg, precision=highest)
    target = initial_norm * hessenberg[0]
    small_factor = jnp.linalg.cholesky(normal_matrix)
    least = triangle_solve(small_factor, triangle_solve(small_factor, target, False), True)
    every_basis = jnp.stack(basis)
    coupled = jnp.dot(coupling, least, precision=highest)
    recycled_term = jnp.dot(coupled, recycled_hat, precision=highest)
    solution = start_point + jnp.dot(least, every_basis[:STEPS], precision=highest) - recycled_term
    residual = start_residual - jnp.dot(
        jnp.dot(hessenberg, least, precision=highest), every_basis, precision=highest
    )
    return (solution.reshape(slot_count, tile_width), residual.reshape(slot_count, tile_width))


def solution(mesh):
    return jax.shard_map(
        local,
        mesh=mesh,
        in_specs=(
            P(("dom", "sub"), None),
            P(None, ("dom", "sub"), None),
            P(None, ("dom", "sub"), None),
            P(("dom", "sub"), None, None, None),
            P(("dom", "sub"), None),
            P(("dom", "sub"), None),
            P(("dom", "sub")),
        ),
        out_specs=(P(("dom", "sub"), None), P(("dom", "sub"), None)),
        check_vma=False,
    )
```

profile of v0, /device:TPU:0, one launch (start us, length us, event | category | flops | bytes accessed | tf_op | source)
XLA Modules:
  0.0 252.3 jit_solution(12142202452177539300)
XLA Ops:
  1.4 0.9 broadcast_multiply_fusion
  2.3 0.2 convolution_bitcast_fusion
  2.5 0.5 copy-done.1
  3.0 0.7 multiply_reduce_fusion.4
  3.8 42.4 %all-reduce.5 = (f32[40,40]{0,1:T(8,128)S(1)}, f32[]{:T(128)}, f32[40]{0:T(128)S(1)}) all-reduce(f32[40,40]{0,1:T(8,128)S(1)} %convolution_bitcast_fusion, f32[]{:T(128)} %get-tuple-element.131, f32[40]{0:T(128)S(1)} %convolution_bitcast_fusion.5), channel_id=1, replica_groups=mesh['dom'=8,'sub'=4] {'dom','sub'}, use_global_device_ids=true, to_apply=%region_0.0 | all-reduce | flops 1641 | bytes 13128 | tf_op jit(solution)/shard_map/psum | solution.py:50
  46.3 3.6 %cholesky.29 = f32[40,40]{1,0:T(8,128)S(1)} custom-call(f32[40,40]{1,0:T(8,128)S(1)} %fusion.13), custom_call_target="Cholesky" | custom-call | tf_op jit(solution)/shard_map/jit(cholesky)/cholesky | solution.py:58
  50.0 0.6 compare_reduce_fusion.4
  50.6 0.7 fusion.8
  51.3 3.1 %custom-call.17 = f32[1,40,40]{1,2,0:T(8,128)S(1)} custom-call(f32[1,40,40]{2,1,0:T(8,128)S(1)} %fusion.8), custom_call_target="InvertDiagBlocksLowerTriangular" | custom-call | tf_op jit(solution)/shard_map/triangular_solve | solution.py:24
  54.3 0.2 fusion
  54.6 0.7 fusion.47
  56.8 5.2 %all-gather = f32[4,2,128]{2,1,0:T(2,128)S(1)} all-gather(f32[1,2,128]{2,1,0:T(2,128)S(1)} %bitcast.252), channel_id=1, replica_groups=mesh['dom'=8,'sub'=4] {'sub'}, dimensions={0}, use_global_device_ids=true | all-gather | bytes 5120 | tf_op jit(solution)/shard_map/all_gather | solution.py:33
  62.0 1.4 collective-permute-start.1
  63.4 4.7 %collective-permute-start = (f32[8,128]{1,0:T(8,128)S(1)}, f32[8,128]{1,0:T(8,128)S(1)}, u32[]{:S(2)}, u32[]{:S(2)}) collective-permute-start(f32[8,128]{1,0:T(8,128)S(1)} %bitcast.262), channel_id=1, source_target_pairs={{0,4},{4,8},{8,12},{12,16},{16,20},{20,24},{24,28},{1,5},{5,9},{9,... | collective-permute-start | bytes 12296 | tf_op jit(solution)/shard_map/ppermute | solution.py:16
  68.2 0.7 copy-done.2
  68.9 0.6 fusion.60
  69.6 0.7 and_reduce_fusion
  70.3 0.2 fusion.3
  70.7 0.7 compare_reduce_fusion.1
  71.4 0.6 gather_fusion
  72.0 0.6 gather_fusion.1
  72.6 1.0 fusion.61
  73.6 0.7 fusion.30
  74.3 0.6 multiply_reduce_fusion.3
  75.0 40.7 %all-reduce.4 = (f32[40]{0:T(128)S(1)}, f32[]{:T(128)}, f32[1]{0:T(128)}) all-reduce(f32[40]{0:T(128)S(1)} %convolution_bitcast_fusion.4, f32[]{:T(128)} %multiply_reduce_fusion.3, f32[1]{0:T(128)} %bitcast.29), channel_id=1, replica_groups=mesh['dom'=8,'sub'=4] {'dom','sub'}, use_global_device_ids=true, to_apply=%region_10.14 | all-reduce | flops 42 | bytes 336 | tf_op jit(solution)/shard_map/psum | solution.py:75
  115.9 1.3 multiply_reduce_fusion.9
  119.8 0.7 fusion.32
  120.5 5.5 %all-gather.1 = f32[4,2,128]{2,1,0:T(2,128)S(1)} all-gather(f32[1,2,128]{2,1,0:T(2,128)S(1)} %bitcast.270), channel_id=1, replica_groups=mesh['dom'=8,'sub'=4] {'sub'}, dimensions={0}, use_global_device_ids=true | all-gather | bytes 5120 | tf_op jit(solution)/shard_map/all_gather | solution.py:33
  126.0 1.3 collective-permute-start.3
  127.2 4.5 %collective-permute-start.2 = (f32[8,128]{1,0:T(8,128)S(1)}, f32[8,128]{1,0:T(8,128)S(1)}, u32[]{:S(2)}, u32[]{:S(2)}) collective-permute-start(f32[8,128]{1,0:T(8,128)S(1)} %bitcast.268), channel_id=1, source_target_pairs={{0,4},{4,8},{8,12},{12,16},{16,20},{20,24},{24,28},{1,5},{5,9},{9,... | collective-permute-start | bytes 12296 | tf_op jit(solution)/shard_map/ppermute | solution.py:16
  131.8 0.6 fusion.59
  132.5 0.6 compare_reduce_fusion.3
  133.1 0.6 compare_reduce_fusion
  133.7 0.6 scatter.30
  134.6 0.6 gather_fusion.2
  135.2 0.6 gather_fusion.3
  135.8 1.0 fusion.62
  136.8 0.7 multiply_reduce_fusion.2
  137.6 0.1 convolution_bitcast_fusion.10
  137.8 41.0 %all-reduce.3 = (f32[40]{0:T(128)S(1)}, f32[2]{0:T(128)S(1)}, f32[]{:T(128)}) all-reduce(f32[40]{0:T(128)S(1)} %convolution_bitcast_fusion.3, f32[2]{0:T(128)S(1)} %convolution_bitcast_fusion.10, f32[]{:T(128)} %get-tuple-element.127), channel_id=1, replica_groups=mesh['dom'=8,'sub'=4] {'dom','sub'}, use_global_device_ids=true, to_apply=%region_16.20 | all-reduce | flops 43 | bytes 344 | tf_op jit(solution)/shard_map/psum | solution.py:75
  178.7 0.7 multiply_reduce_fusion.7
  179.7 1.2 multiply_reduce_fusion.8
  182.9 5.5 %all-gather.2 = f32[4,2,128]{2,1,0:T(2,128)S(1)} all-gather(f32[1,2,128]{2,1,0:T(2,128)S(1)} %bitcast.278), channel_id=1, replica_groups=mesh['dom'=8,'sub'=4] {'sub'}, dimensions={0}, use_global_device_ids=true | all-gather | bytes 5120 | tf_op jit(solution)/shard_map/all_gather | solution.py:33
  188.4 1.3 collective-permute-start.5
  189.7 4.5 %collective-permute-start.4 = (f32[8,128]{1,0:T(8,128)S(1)}, f32[8,128]{1,0:T(8,128)S(1)}, u32[]{:S(2)}, u32[]{:S(2)}) collective-permute-start(f32[8,128]{1,0:T(8,128)S(1)} %bitcast.265), channel_id=1, source_target_pairs={{0,4},{4,8},{8,12},{12,16},{16,20},{20,24},{24,28},{1,5},{5,9},{9,... | collective-permute-start | bytes 12296 | tf_op jit(solution)/shard_map/ppermute | solution.py:16
  194.2 1.9 broadcast_select_fusion.6
  196.1 1.3 scatter.34
  197.7 0.6 gather_fusion.4
  198.3 0.6 gather_fusion.5
  199.0 1.0 fusion.63
  199.9 0.7 multiply_reduce_fusion.1
  200.7 0.1 convolution_bitcast_fusion.2
  200.9 40.7 %all-reduce.2 = (f32[40]{0:T(128)S(1)}, f32[3]{0:T(128)S(1)}, f32[]{:T(128)}) all-reduce(f32[40]{0:T(128)S(1)} %convolution_bitcast_fusion.1, f32[3]{0:T(128)S(1)} %convolution_bitcast_fusion.2, f32[]{:T(128)} %get-tuple-element.125), channel_id=1, replica_groups=mesh['dom'=8,'sub'=4] {'dom','sub'}, use_global_device_ids=true, to_apply=%region_23.27 | all-reduce | flops 44 | bytes 352 | tf_op jit(solution)/shard_map/psum | solution.py:75
  241.5 0.6 multiply_reduce_fusion.5
  242.1 2.0 broadcast_select_fusion.5
  244.1 1.4 scatter.36
  245.5 0.6 multiply_reduce_fusion.6
  248.5 0.1 fusion.57
  248.8 0.3 cholesky.61
  249.1 0.6 compare_reduce_fusion.2
  249.7 0.6 fusion.22
  250.4 0.3 custom-call.18
  251.4 0.1 fusion.65
  251.7 0.6 subtract_bitcast_fusion
  (69 shorter events, 3.8 us)
Async XLA Ops:
  0.6 72.0 %copy-start = (f32[2,8,128,128]{3,2,1,0:T(8,128)S(1)}, f32[2,8,128,128]{3,2,1,0:T(8,128)}, u32[]{:S(2)}) copy-start(f32[2,8,128,128]{3,2,1,0:T(8,128)} %param.34) | copy-start | bytes 3145732
  2.3 0.7 copy-start.1
  62.0 6.2 %copy-start.3 = (s32[1,4]{1,0:T(1,128)S(1)}, s32[1,4]{1,0:T(1,128)}, u32[]{:S(2)}) copy-start(s32[1,4]{1,0:T(1,128)} %param.36) | copy-start | bytes 52
  62.0 9.4 %collective-permute-start.1 = (f32[8,128]{1,0:T(8,128)S(1)}, f32[8,128]{1,0:T(8,128)S(1)}, u32[]{:S(2)}, u32[]{:S(2)}) collective-permute-start(f32[8,128]{1,0:T(8,128)S(1)} %bitcast.261), channel_id=1, source_target_pairs={{4,0},{8,4},{12,8},{16,12},{20,16},{24,20},{28,24},{5,1},{9,5},{13... | collective-permute-start | bytes 12296 | tf_op jit(solution)/shard_map/ppermute | solution.py:17
  63.4 8.0 %collective-permute-start = (f32[8,128]{1,0:T(8,128)S(1)}, f32[8,128]{1,0:T(8,128)S(1)}, u32[]{:S(2)}, u32[]{:S(2)}) collective-permute-start(f32[8,128]{1,0:T(8,128)S(1)} %bitcast.262), channel_id=1, source_target_pairs={{0,4},{4,8},{8,12},{12,16},{16,20},{20,24},{24,28},{1,5},{5,9},{9,... | collective-permute-start | bytes 12296 | tf_op jit(solution)/shard_map/ppermute | solution.py:16
  68.1 0.7 copy-start.2
  68.9 0.7 copy-start.4
  126.0 8.6 %collective-permute-start.3 = (f32[8,128]{1,0:T(8,128)S(1)}, f32[8,128]{1,0:T(8,128)S(1)}, u32[]{:S(2)}, u32[]{:S(2)}) collective-permute-start(f32[8,128]{1,0:T(8,128)S(1)} %bitcast.267), channel_id=1, source_target_pairs={{4,0},{8,4},{12,8},{16,12},{20,16},{24,20},{28,24},{5,1},{9,5},{13... | collective-permute-start | bytes 12296 | tf_op jit(solution)/shard_map/ppermute | solution.py:17
  127.2 7.3 %collective-permute-start.2 = (f32[8,128]{1,0:T(8,128)S(1)}, f32[8,128]{1,0:T(8,128)S(1)}, u32[]{:S(2)}, u32[]{:S(2)}) collective-permute-start(f32[8,128]{1,0:T(8,128)S(1)} %bitcast.268), channel_id=1, source_target_pairs={{0,4},{4,8},{8,12},{12,16},{16,20},{20,24},{24,28},{1,5},{5,9},{9,... | collective-permute-start | bytes 12296 | tf_op jit(solution)/shard_map/ppermute | solution.py:16
  188.4 9.2 %collective-permute-start.5 = (f32[8,128]{1,0:T(8,128)S(1)}, f32[8,128]{1,0:T(8,128)S(1)}, u32[]{:S(2)}, u32[]{:S(2)}) collective-permute-start(f32[8,128]{1,0:T(8,128)S(1)} %bitcast.264), channel_id=1, source_target_pairs={{4,0},{8,4},{12,8},{16,12},{20,16},{24,20},{28,24},{5,1},{9,5},{13... | collective-permute-start | bytes 12296 | tf_op jit(solution)/shard_map/ppermute | solution.py:17
  189.7 8.0 %collective-permute-start.4 = (f32[8,128]{1,0:T(8,128)S(1)}, f32[8,128]{1,0:T(8,128)S(1)}, u32[]{:S(2)}, u32[]{:S(2)}) collective-permute-start(f32[8,128]{1,0:T(8,128)S(1)} %bitcast.265), channel_id=1, source_target_pairs={{0,4},{4,8},{8,12},{12,16},{16,20},{20,24},{24,28},{1,5},{5,9},{9,... | collective-permute-start | bytes 12296 | tf_op jit(solution)/shard_map/ppermute | solution.py:16
where the time goes:
time: 254 us; the launch traced here: 252 us
  blocking collectives  181 us (71%)
  other arithmetic  26.9 us (11%)
  starting transfers between devices  17.8 us (7%)
  local copies, waits for them, and re-layouts  9.88 us (4%)
  between operations  9.6 us (4%)
  matrix products  7.11 us (3%)
    psum x3, blocking collectives, local(): lax.psum((local_images, jnp.dot(stacked, image_now, precision=highest), j...  122 us
    psum x1, blocking collectives, local(): lax.psum((jnp.dot(images_flat, images_flat.T, precision=highest), jnp.dot...  42.4 us
    all_gather x3, blocking collectives, multiply(): gathered = lax.all_gather(vector, 'sub', axis=0, tiled=True)  16.2 us
    ppermute x3, starting transfers between devices, padded(): before = lax.ppermute(last, axis, up)  13.8 us
    another operation x7, other arithmetic  6.56 us
  transfers between devices with their start and end apart: 6, of which 0 were waited for; matrix products, arithmetic and copies ran while one was open for 3% of the time, Pallas kernels for 0%

commit v1 on v0

--- a/solution.py
+++ b/solution.py
@@ -30,7 +30,18 @@
 def multiply(vector, matrix_tiles, tile_columns, ghost_codes):
     slot_count = vector.shape[0]
     group_size = lax.axis_size("sub") * slot_count
-    gathered = lax.all_gather(vector, "sub", axis=0, tiled=True)
+    n_dev_all = jax.lax.axis_size("sub")
+    o_now = [(w - 1, w) for w in range(1, n_dev_all)] + [(n_dev_all - 1, 0)]
+    v_now = vector
+    buffers = [v_now]
+    for _ in range(n_dev_all - 1):
+        v_now = jax.lax.ppermute(v_now, "sub", o_now)
+        buffers += [v_now]
+    gathered = jnp.roll(
+        jnp.concatenate([*reversed(buffers)], axis=0),
+        (jax.lax.axis_index("sub") + 1) * v_now.shape[0],
+        axis=0,
+    )
     nearby = padded(gathered, (("dom", 0),), group_size)
     ghosts = jnp.take(nearby, ghost_codes, axis=0)
     extended = jnp.concatenate([vector, ghosts], axis=0)

time: 254 us -> 266 us (1.047)
  waiting for transfers between devices: 0.02 us -> 22 us
  blocking collectives: 181 us -> 169 us
    ppermute x0 -> x9, waiting for transfers between devices: none -> 21.3 us  [multiply(): v_now = jax.lax.ppermute(v_now, 'sub', o_now)]
    all_gather x3 -> x0, blocking collectives: 16.2 us -> none  [multiply(): gathered = lax.all_gather(vector, 'sub', axis=0, tiled=True)]
    psum x3, blocking collectives: 122 us -> 126 us  [local(): lax.psum((local_images, jnp.dot(stacked, image_now, precision=highest), j...]
  transfers between devices with their start and end apart: 6 -> 15, of which waited for: 0 -> 10; matrix products, arithmetic and copies ran while one was open for 3% -> 3% of each run, Pallas kernels for 0% -> 0%
where the time goes in v1:
time: 266 us; the launch traced here: 264 us
  blocking collectives  169 us (64%)
  other arithmetic  27 us (10%)
  waiting for transfers between devices  22 us (8%)
  starting transfers between devices  19.7 us (7%)
  local copies, waits for them, and re-layouts  10.5 us (4%)
  between operations  9.55 us (4%)
  matrix products  7.11 us (3%)
    psum x3, blocking collectives, local(): lax.psum((local_images, jnp.dot(stacked, image_now, precision=highest), j...  126 us
    psum x1, blocking collectives, local(): lax.psum((jnp.dot(images_flat, images_flat.T, precision=highest), jnp.dot...  42.4 us
    ppermute x9, waiting for transfers between devices, multiply(): v_now = jax.lax.ppermute(v_now, 'sub', o_now)  21.3 us
    ppermute x3, starting transfers between devices, padded(): before = lax.ppermute(last, axis, up)  14.4 us
    another operation x7, other arithmetic  6.5 us
  transfers between devices with their start and end apart: 15, of which 10 were waited for; matrix products, arithmetic and copies ran while one was open for 3% of the time, Pallas kernels for 0%

profile of v1, /device:TPU:0, one launch (start us, length us, event | category | flops | bytes accessed | tf_op | source)
XLA Modules:
  0.0 264.3 jit_solution(1508189952984742930)
XLA Ops:
  1.4 0.9 broadcast_multiply_fusion
  2.5 0.5 copy-done.1
  3.0 0.7 multiply_reduce_fusion.4
  3.8 42.4 %all-reduce.5 = (f32[40,40]{0,1:T(8,128)S(1)}, f32[]{:T(128)}, f32[40]{0:T(128)S(1)}) all-reduce(f32[40,40]{0,1:T(8,128)S(1)} %convolution_bitcast_fusion, f32[]{:T(128)} %get-tuple-element.132, f32[40]{0:T(128)S(1)} %convolution_bitcast_fusion.5), channel_id=1, replica_groups=mesh['dom'=8,'sub'=4] {'dom','sub'}, use_global_device_ids=true, to_apply=%region_0.0 | all-reduce | flops 1641 | bytes 13128 | tf_op jit(solution)/shard_map/psum | solution.py:61
  46.3 3.6 %cholesky.29 = f32[40,40]{1,0:T(8,128)S(1)} custom-call(f32[40,40]{1,0:T(8,128)S(1)} %fusion.13), custom_call_target="Cholesky" | custom-call | tf_op jit(solution)/shard_map/jit(cholesky)/cholesky | solution.py:69
  50.0 0.6 compare_reduce_fusion.4
  50.6 0.7 fusion.8
  51.3 3.1 %custom-call.17 = f32[1,40,40]{1,2,0:T(8,128)S(1)} custom-call(f32[1,40,40]{2,1,0:T(8,128)S(1)} %fusion.8), custom_call_target="InvertDiagBlocksLowerTriangular" | custom-call | tf_op jit(solution)/shard_map/triangular_solve | solution.py:24
  54.6 0.7 fusion.68
  56.9 0.6 copy-done.2
  57.5 0.6 copy-done.3
  58.2 1.7 collective-permute-done
  59.9 3.0 %collective-permute-done.1 = f32[2,128]{1,0:T(2,128)S(1)} collective-permute-done((f32[2,128]{1,0:T(2,128)S(1)}, f32[2,128]{1,0:T(2,128)S(1)}, u32[]{:S(2)}, u32[]{:S(2)}) %collective-permute-start.1) | collective-permute-done | bytes 1056 | tf_op jit(solution)/shard_map/ppermute | solution.py:38
  63.0 2.9 %collective-permute-done.2 = f32[2,128]{1,0:T(2,128)S(1)} collective-permute-done((f32[2,128]{1,0:T(2,128)S(1)}, f32[2,128]{1,0:T(2,128)S(1)}, u32[]{:S(2)}, u32[]{:S(2)}) %collective-permute-start.2) | collective-permute-done | bytes 1056 | tf_op jit(solution)/shard_map/ppermute | solution.py:38
  65.9 1.3 collective-permute-start.4
  67.2 4.8 %collective-permute-start.3 = (f32[8,128]{1,0:T(8,128)S(1)}, f32[8,128]{1,0:T(8,128)S(1)}, u32[]{:S(2)}, u32[]{:S(2)}) collective-permute-start(f32[8,128]{1,0:T(8,128)S(1)} %fusion.31), channel_id=1, source_target_pairs={{0,4},{4,8},{8,12},{12,16},{16,20},{20,24},{24,28},{1,5},{5,9},{9,... | collective-permute-start | bytes 12296 | tf_op jit(solution)/shard_map/ppermute | solution.py:16
  72.0 0.6 compare_reduce_fusion.1
  72.7 0.7 collective-permute-done.3
  73.3 0.6 gather_fusion
  74.0 0.6 gather_fusion.1
  74.6 1.0 fusion.82
  75.6 0.7 fusion.51
  76.3 0.6 multiply_reduce_fusion.3
  77.0 42.7 %all-reduce.4 = (f32[40]{0:T(128)S(1)}, f32[]{:T(128)}, f32[1]{0:T(128)}) all-reduce(f32[40]{0:T(128)S(1)} %convolution_bitcast_fusion.4, f32[]{:T(128)} %multiply_reduce_fusion.3, f32[1]{0:T(128)} %bitcast.27), channel_id=1, replica_groups=mesh['dom'=8,'sub'=4] {'dom','sub'}, use_global_device_ids=true, to_apply=%region_10.15 | all-reduce | flops 42 | bytes 336 | tf_op jit(solution)/shard_map/psum | solution.py:86
  119.8 1.2 multiply_reduce_fusion.9
  123.7 0.7 fusion.53
  124.5 3.0 %collective-permute-done.5 = f32[2,128]{1,0:T(2,128)S(1)} collective-permute-done((f32[2,128]{1,0:T(2,128)S(1)}, f32[2,128]{1,0:T(2,128)S(1)}, u32[]{:S(2)}, u32[]{:S(2)}) %collective-permute-start.5) | collective-permute-done | bytes 1056 | tf_op jit(solution)/shard_map/ppermute | solution.py:38
  128.0 2.5 collective-permute-done.6
  130.9 2.6 collective-permute-done.7
  133.5 1.3 collective-permute-start.9
  134.8 4.8 %collective-permute-start.8 = (f32[8,128]{1,0:T(8,128)S(1)}, f32[8,128]{1,0:T(8,128)S(1)}, u32[]{:S(2)}, u32[]{:S(2)}) collective-permute-start(f32[8,128]{1,0:T(8,128)S(1)} %fusion.24), channel_id=1, source_target_pairs={{0,4},{4,8},{8,12},{12,16},{16,20},{20,24},{24,28},{1,5},{5,9},{9,... | collective-permute-start | bytes 12296 | tf_op jit(solution)/shard_map/ppermute | solution.py:16
  139.6 0.7 and_reduce_fusion
  140.3 0.6 compare_reduce_fusion
  141.0 0.6 gather_fusion.2
  141.6 0.6 gather_fusion.3
  142.3 1.0 fusion.83
  143.2 0.8 multiply_reduce_fusion.2
  144.3 42.5 %all-reduce.3 = (f32[40]{0:T(128)S(1)}, f32[2]{0:T(128)S(1)}, f32[]{:T(128)}) all-reduce(f32[40]{0:T(128)S(1)} %convolution_bitcast_fusion.3, f32[2]{0:T(128)S(1)} %convolution_bitcast_fusion.10, f32[]{:T(128)} %get-tuple-element.128), channel_id=1, replica_groups=mesh['dom'=8,'sub'=4] {'dom','sub'}, use_global_device_ids=true, to_apply=%region_16.21 | all-reduce | flops 43 | bytes 344 | tf_op jit(solution)/shard_map/psum | solution.py:86
  186.7 0.7 multiply_reduce_fusion.7
  187.7 1.2 multiply_reduce_fusion.8
  190.9 0.6 fusion.81
  191.5 2.4 collective-permute-done.10
  193.8 0.3 collective-permute-start.11
  194.2 2.7 %collective-permute-done.11 = f32[2,128]{1,0:T(2,128)S(1)} collective-permute-done((f32[2,128]{1,0:T(2,128)S(1)}, f32[2,128]{1,0:T(2,128)S(1)}, u32[]{:S(2)}, u32[]{:S(2)}) %collective-permute-start.11) | collective-permute-done | bytes 1056 | tf_op jit(solution)/shard_map/ppermute | solution.py:38
  197.2 0.6 fusion.80
  197.8 0.6 compare_reduce_fusion.3
  198.4 0.6 scatter.30
  199.2 0.6 collective-permute-done.12
  199.9 1.3 collective-permute-start.14
  201.2 4.8 %collective-permute-start.13 = (f32[8,128]{1,0:T(8,128)S(1)}, f32[8,128]{1,0:T(8,128)S(1)}, u32[]{:S(2)}, u32[]{:S(2)}) collective-permute-start(f32[8,128]{1,0:T(8,128)S(1)} %fusion.17), channel_id=1, source_target_pairs={{0,4},{4,8},{8,12},{12,16},{16,20},{20,24},{24,28},{1,5},{5,9},{9,... | collective-permute-start | bytes 12296 | tf_op jit(solution)/shard_map/ppermute | solution.py:16
  206.0 1.9 broadcast_select_fusion.6
  207.9 1.4 scatter.34
  209.4 0.6 gather_fusion.4
  210.1 0.6 gather_fusion.5
  210.7 1.0 fusion.84
  211.7 0.7 multiply_reduce_fusion.1
  212.6 40.9 %all-reduce.2 = (f32[40]{0:T(128)S(1)}, f32[3]{0:T(128)S(1)}, f32[]{:T(128)}) all-reduce(f32[40]{0:T(128)S(1)} %convolution_bitcast_fusion.1, f32[3]{0:T(128)S(1)} %convolution_bitcast_fusion.2, f32[]{:T(128)} %get-tuple-element.126), channel_id=1, replica_groups=mesh['dom'=8,'sub'=4] {'dom','sub'}, use_global_device_ids=true, to_apply=%region_23.28 | all-reduce | flops 44 | bytes 352 | tf_op jit(solution)/shard_map/psum | solution.py:86
  253.6 0.6 multiply_reduce_fusion.5
  254.2 2.0 broadcast_select_fusion.5
  256.2 1.4 scatter.36
  257.6 0.6 multiply_reduce_fusion.6
  261.2 0.6 compare_reduce_fusion.2
  261.8 0.6 fusion.43
  263.8 0.6 subtract_bitcast_fusion
  (87 shorter events, 6.7 us)
Async XLA Ops:
  0.6 74.0 %copy-start = (f32[2,8,128,128]{3,2,1,0:T(8,128)S(1)}, f32[2,8,128,128]{3,2,1,0:T(8,128)}, u32[]{:S(2)}) copy-start(f32[2,8,128,128]{3,2,1,0:T(8,128)} %param.36) | copy-start | bytes 3145732
  2.3 0.7 copy-start.1
  56.8 0.7 copy-start.2
  56.8 3.1 %collective-permute-start = (f32[2,128]{1,0:T(2,128)S(1)}, f32[2,128]{1,0:T(2,128)S(1)}, u32[]{:S(2)}, u32[]{:S(2)}) collective-permute-start(f32[2,128]{1,0:T(2,128)S(1)} %bitcast.246), channel_id=1, source_target_pairs={{0,1},{1,2},{2,3},{3,0},{4,5},{5,6},{6,7},{7,4},{8,9},{9,10},{10,1... | collective-permute-start | bytes 3080 | tf_op jit(solution)/shard_map/ppermute | solution.py:38
  57.5 0.7 copy-start.3
  59.9 3.0 %collective-permute-start.1 = (f32[2,128]{1,0:T(2,128)S(1)}, f32[2,128]{1,0:T(2,128)S(1)}, u32[]{:S(2)}, u32[]{:S(2)}) collective-permute-start(f32[2,128]{1,0:T(2,128)S(1)} %collective-permute-done), channel_id=1, source_target_pairs={{0,1},{1,2},{2,3},{3,0},{4,5},{5,6},{6,7},{7,4},{8,9},{9,10},{10,1... | collective-permute-start | bytes 3080 | tf_op jit(solution)/shard_map/ppermute | solution.py:38
  62.9 3.0 %collective-permute-start.2 = (f32[2,128]{1,0:T(2,128)S(1)}, f32[2,128]{1,0:T(2,128)S(1)}, u32[]{:S(2)}, u32[]{:S(2)}) collective-permute-start(f32[2,128]{1,0:T(2,128)S(1)} %collective-permute-done.1), channel_id=1, source_target_pairs={{0,1},{1,2},{2,3},{3,0},{4,5},{5,6},{6,7},{7,4},{8,9},{9,10},{10,1... | collective-permute-start | bytes 3080 | tf_op jit(solution)/shard_map/ppermute | solution.py:38
  65.9 6.8 %collective-permute-start.4 = (f32[8,128]{1,0:T(8,128)S(1)}, f32[8,128]{1,0:T(8,128)S(1)}, u32[]{:S(2)}, u32[]{:S(2)}) collective-permute-start(f32[8,128]{1,0:T(8,128)S(1)} %fusion.31), channel_id=1, source_target_pairs={{4,0},{8,4},{12,8},{16,12},{20,16},{24,20},{28,24},{5,1},{9,5},{13... | collective-permute-start | bytes 12296 | tf_op jit(solution)/shard_map/ppermute | solution.py:17
  67.2 6.1 %collective-permute-start.3 = (f32[8,128]{1,0:T(8,128)S(1)}, f32[8,128]{1,0:T(8,128)S(1)}, u32[]{:S(2)}, u32[]{:S(2)}) collective-permute-start(f32[8,128]{1,0:T(8,128)S(1)} %fusion.31), channel_id=1, source_target_pairs={{0,4},{4,8},{8,12},{12,16},{16,20},{20,24},{24,28},{1,5},{5,9},{9,... | collective-permute-start | bytes 12296 | tf_op jit(solution)/shard_map/ppermute | solution.py:16
  124.4 3.1 %collective-permute-start.5 = (f32[2,128]{1,0:T(2,128)S(1)}, f32[2,128]{1,0:T(2,128)S(1)}, u32[]{:S(2)}, u32[]{:S(2)}) collective-permute-start(f32[2,128]{1,0:T(2,128)S(1)} %bitcast.256), channel_id=1, source_target_pairs={{0,1},{1,2},{2,3},{3,0},{4,5},{5,6},{6,7},{7,4},{8,9},{9,10},{10,1... | collective-permute-start | bytes 3080 | tf_op jit(solution)/shard_map/ppermute | solution.py:38
  127.5 3.0 %collective-permute-start.6 = (f32[2,128]{1,0:T(2,128)S(1)}, f32[2,128]{1,0:T(2,128)S(1)}, u32[]{:S(2)}, u32[]{:S(2)}) collective-permute-start(f32[2,128]{1,0:T(2,128)S(1)} %collective-permute-done.5), channel_id=1, source_target_pairs={{0,1},{1,2},{2,3},{3,0},{4,5},{5,6},{6,7},{7,4},{8,9},{9,10},{10,1... | collective-permute-start | bytes 3080 | tf_op jit(solution)/shard_map/ppermute | solution.py:38
  130.5 3.0 %collective-permute-start.7 = (f32[2,128]{1,0:T(2,128)S(1)}, f32[2,128]{1,0:T(2,128)S(1)}, u32[]{:S(2)}, u32[]{:S(2)}) collective-permute-start(f32[2,128]{1,0:T(2,128)S(1)} %collective-permute-done.6), channel_id=1, source_target_pairs={{0,1},{1,2},{2,3},{3,0},{4,5},{5,6},{6,7},{7,4},{8,9},{9,10},{10,1... | collective-permute-start | bytes 3080 | tf_op jit(solution)/shard_map/ppermute | solution.py:38
  130.9 8.7 %copy-start.4 = (s32[2]{0:T(128)S(1)}, s32[2]{0:T(128)}, u32[]{:S(2)}) copy-start(s32[2]{0:T(128)} %constant.360.clone.1) | copy-start | bytes 28
  133.5 7.5 %collective-permute-start.9 = (f32[8,128]{1,0:T(8,128)S(1)}, f32[8,128]{1,0:T(8,128)S(1)}, u32[]{:S(2)}, u32[]{:S(2)}) collective-permute-start(f32[8,128]{1,0:T(8,128)S(1)} %fusion.24), channel_id=1, source_target_pairs={{4,0},{8,4},{12,8},{16,12},{20,16},{24,20},{28,24},{5,1},{9,5},{13... | collective-permute-start | bytes 12296 | tf_op jit(solution)/shard_map/ppermute | solution.py:17
  134.8 6.2 %collective-permute-start.8 = (f32[8,128]{1,0:T(8,128)S(1)}, f32[8,128]{1,0:T(8,128)S(1)}, u32[]{:S(2)}, u32[]{:S(2)}) collective-permute-start(f32[8,128]{1,0:T(8,128)S(1)} %fusion.24), channel_id=1, source_target_pairs={{0,4},{4,8},{8,12},{12,16},{16,20},{20,24},{24,28},{1,5},{5,9},{9,... | collective-permute-start | bytes 12296 | tf_op jit(solution)/shard_map/ppermute | solution.py:16
  190.8 3.1 %collective-permute-start.10 = (f32[2,128]{1,0:T(2,128)S(1)}, f32[2,128]{1,0:T(2,128)S(1)}, u32[]{:S(2)}, u32[]{:S(2)}) collective-permute-start(f32[2,128]{1,0:T(2,128)S(1)} %bitcast.265), channel_id=1, source_target_pairs={{0,1},{1,2},{2,3},{3,0},{4,5},{5,6},{6,7},{7,4},{8,9},{9,10},{10,1... | collective-permute-start | bytes 3080 | tf_op jit(solution)/shard_map/ppermute | solution.py:38
  193.8 3.0 %collective-permute-start.11 = (f32[2,128]{1,0:T(2,128)S(1)}, f32[2,128]{1,0:T(2,128)S(1)}, u32[]{:S(2)}, u32[]{:S(2)}) collective-permute-start(f32[2,128]{1,0:T(2,128)S(1)} %collective-permute-done.10), channel_id=1, source_target_pairs={{0,1},{1,2},{2,3},{3,0},{4,5},{5,6},{6,7},{7,4},{8,9},{9,10},{10,1... | collective-permute-start | bytes 3080 | tf_op jit(solution)/shard_map/ppermute | solution.py:38
  196.8 3.0 %collective-permute-start.12 = (f32[2,128]{1,0:T(2,128)S(1)}, f32[2,128]{1,0:T(2,128)S(1)}, u32[]{:S(2)}, u32[]{:S(2)}) collective-permute-start(f32[2,128]{1,0:T(2,128)S(1)} %collective-permute-done.11), channel_id=1, source_target_pairs={{0,1},{1,2},{2,3},{3,0},{4,5},{5,6},{6,7},{7,4},{8,9},{9,10},{10,1... | collective-permute-start | bytes 3080 | tf_op jit(solution)/shard_map/ppermute | solution.py:38
  199.9 9.5 %collective-permute-start.14 = (f32[8,128]{1,0:T(8,128)S(1)}, f32[8,128]{1,0:T(8,128)S(1)}, u32[]{:S(2)}, u32[]{:S(2)}) collective-permute-start(f32[8,128]{1,0:T(8,128)S(1)} %fusion.17), channel_id=1, source_target_pairs={{4,0},{8,4},{12,8},{16,12},{20,16},{24,20},{28,24},{5,1},{9,5},{13... | collective-permute-start | bytes 12296 | tf_op jit(solution)/shard_map/ppermute | solution.py:17
  201.2 8.2 %collective-permute-start.13 = (f32[8,128]{1,0:T(8,128)S(1)}, f32[8,128]{1,0:T(8,128)S(1)}, u32[]{:S(2)}, u32[]{:S(2)}) collective-permute-start(f32[8,128]{1,0:T(8,128)S(1)} %fusion.17), channel_id=1, source_target_pairs={{0,4},{4,8},{8,12},{12,16},{16,20},{20,24},{24,28},{1,5},{5,9},{9,... | collective-permute-start | bytes 12296 | tf_op jit(solution)/shard_map/ppermute | solution.py:16
